TPU v7x, 32 devices: a whole 2x2x4 slice. The times are simulated.
32 devices in a mesh: region: 8 (over z, x), member: 4 (over y, core).
Axes of the slice: x: 2, y: 2, z: 4, core: 2. Of those that a mesh axis runs over, the one named last changes fastest.
Arguments:
- ensemble: bfloat16 [40, 131072], P('member', 'region'), may hold values from -6 to 6
- obs_value: float32 [1024, 128], P(('region', 'member')), may hold values from -8 to 8
- obs_var: float32 [1024, 128], P(('region', 'member')), may hold values from 0.1 to 1
- obs_point: int32 [1024, 128], P(('region', 'member')), may hold values from 0 to 16383
- owned_blocks: int32 [1024], P('region'), may hold values from 0 to 1023, each once
- infl_mean: float32 [1024], replicated, may hold values from 0.6 to 1.6
- infl_var: float32 [1024], replicated, may hold values from 0.0001 to 0.1
Outputs:
- inflated: bfloat16 [40, 131072], P('member', 'region')
- infl_post: float32 [1024], P(('region', 'member'))
Inputs may be any that keep to these rules, and one draw needn't show every extreme that they name: `obs_point`: index among the 16384 points of the observation's region; the observation belongs to the block of that point's slot. `owned_blocks`: every block id appears exactly once.
All inputs are finite; a program needn't handle non-finite values.
Results may differ from a plain program's by a relative error of at most 0.001.
Values sent between devices are 32-bit elements; how exact they have to be, the bound alone decides.
A program may use at most 64 MiB of HBM per device.

v0:
```python
import jax
import jax.numpy as jnp
from jax import lax
from jax.sharding import PartitionSpec as P


def posterior(sums, prior_mean, prior_var):
    innov_sum = sums[0]
    spread_sum = sums[1]
    error_sum = sums[2]
    spread_spread = sums[3]
    spread_error = sums[4]
    error_error = sums[5]
    weight_var = (
        2.0 * prior_mean * prior_mean * (1.0 + spread_spread)
        + 4.0 * prior_mean * spread_error
        + 2.0 * error_error
    )
    value = (prior_mean * weight_var + prior_var * spread_sum * (innov_sum - error_sum)) / (
        weight_var + prior_var * spread_sum * spread_sum
    )
    return jnp.maximum(value, 1.0)


def bin_slots(innovation, spread, errors, slot_of, slots):
    count = innovation.shape[0]
    width = min(count, 2048)
    while count % width != 0:
        width = width // 2
    blocks = count // width
    inno = innovation.reshape(blocks, width)
    sprd = spread.reshape(blocks, width)
    errs = errors.reshape(blocks, width)
    columns = jnp.stack([inno * inno, sprd, errs, sprd * sprd, sprd * errs, errs * errs], 1)
    labels = slot_of.reshape(blocks, width)
    slot_ids = jnp.arange(slots, dtype=jnp.int32)

    def one_block(carry, pair):
        block_cols, block_labels = pair
        onehot = (block_labels[:, None] == slot_ids[None, :]).astype(jnp.float32)
        return (
            carry
            + jnp.dot(
                block_cols,
                onehot,
                precision=lax.Precision.HIGHEST,
                preferred_element_type=jnp.float32,
            ),
            None,
        )

    total, unused = lax.scan(one_block, jnp.zeros((6, slots), jnp.float32), (columns, labels))
    return total


def body(ensemble, obs_value, obs_var, obs_point, owned_blocks, infl_mean, infl_var):
    members = ensemble.shape[0] * lax.axis_size("member")
    wide = ensemble.astype(jnp.float32)
    local_total = jnp.sum(wide, 0)
    local_square = jnp.sum(wide * wide, 0)
    own_points = obs_point.reshape(-1)
    point_total, point_square = lax.psum((local_total, local_square), "member")
    point_mean = point_total / members
    at_square = point_square[own_points]
    at_mean = point_mean[own_points]
    spread = (at_square - members * at_mean * at_mean) / (members - 1)
    innovation = obs_value.reshape(-1) - at_mean
    errors = obs_var.reshape(-1)
    slots = owned_blocks.shape[0]
    span = point_mean.shape[0] // slots
    slot_of = own_points // span
    slot_sums = bin_slots(innovation, spread, errors, slot_of, slots)
    num_blocks = infl_mean.shape[0]
    share = num_blocks // lax.axis_size(("region", "member"))
    first = lax.axis_index(("region", "member")) * share
    placed_sums = jnp.zeros((6, num_blocks), jnp.float32).at[:, owned_blocks].set(slot_sums)
    totals = lax.psum(placed_sums, ("region", "member"))
    lambda_all = posterior(totals, infl_mean, infl_var)
    lambda_mine = lax.dynamic_slice_in_dim(lambda_all, first, share)
    lambda_owned = lambda_all[owned_blocks]
    factor = jnp.sqrt(lambda_owned)[None, :, None]
    mean_slots = point_mean.reshape(1, slots, -1)
    shaped = wide.reshape(wide.shape[0], slots, -1)
    inflated = (
        (mean_slots + factor * (shaped - mean_slots)).astype(jnp.bfloat16).reshape(ensemble.shape)
    )
    return (inflated, lambda_mine)


def solution(mesh):
    placed = (
        P("member", "region"),
        P(("region", "member"), None),
        P(("region", "member"), None),
        P(("region", "member"), None),
        P("region"),
        P(),
        P(),
    )
    return jax.shard_map(
        body,
        mesh=mesh,
        in_specs=placed,
        out_specs=(P("member", "region"), P(("region", "member"))),
        check_vma=False,
    )
```

profile of v0, /device:TPU:0, one launch (start us, length us, event | category | flops | bytes accessed | tf_op | source)
XLA Modules:
  0.0 151.9 jit_solution(3200294530436090924)
XLA Ops:
  7.2 0.0 all-reduce.3.cloned.1.call-start
  7.2 2.2 %fusion.6 = (f32[16384]{0:T(1024)}, f32[16384]{0:T(1024)}) fusion(bf16[10,16384]{1,0:T(8,128)(2,1)} %param.9), kind=kLoop, calls=%fused_computation.15 | loop fusion | flops 622592 | bytes 458752 | tf_op jit(solution)/shard_map/reduce_sum | solution.py:60
  9.4 0.0 all-reduce.3.cloned.1.call-update
  9.4 0.7 copy-done.3
  10.2 0.0 copy-start.7
  10.2 0.6 copy-done.7
  10.9 34.6 %all-reduce.3.cloned.1.call-done = (f32[16384]{0:T(1024)}, f32[16384]{0:T(1024)}) async-done(((f32[16384]{0:T(1024)}, f32[16384]{0:T(1024)}), (f32[16384]{0:T(1024)}, f32[16384]{0:T(1024)})) %all-reduce.3.cloned.1.call-update) | async-done | bytes 131088 | tf_op jit(solution)/shard_map/psum | solution.py:62
  45.5 0.8 broadcast_multiply_fusion
  46.4 23.0 %gather_fusion = f32[4096]{0:T(1024)S(1)} fusion(f32[16384]{0:T(1024)S(1)} %broadcast_multiply_fusion, s32[4096]{0:T(1024)S(1)} %broadcast_clamp_fusion), kind=kCustom, calls=%fused_computation | custom fusion | bytes 49152 | tf_op jit(solution)/shard_map/gather | solution.py:65
  69.4 0.0 copy-done
  69.4 0.0 copy-start.2
  69.4 0.0 copy-start.4
  69.4 23.0 %gather_fusion.1 = f32[4096]{0:T(1024)S(1)} fusion(f32[16384]{0:T(1024)S(1)} %copy-done, s32[4096]{0:T(1024)S(1)} %broadcast_clamp_fusion), kind=kCustom, calls=%fused_computation.1 | custom fusion | bytes 49152 | tf_op jit(solution)/shard_map/gather | solution.py:64
  92.5 0.1 fusion.20
  92.6 0.2 stack.2
  92.7 1.2 while.11
  92.8 0.6 convolution_add_fusion.2
  93.4 0.6 convolution_add_fusion.2
  94.0 0.1 copy.10
  94.1 1.0 scatter_custom_fusion
  95.1 45.8 %psum.23 = f32[6,1024]{0,1:T(8,128)S(1)} all-reduce(f32[6,1024]{0,1:T(8,128)S(1)} %scatter_custom_fusion), channel_id=1, replica_groups=mesh['region'=8,'member'=4] {'region','member'}, use_global_device_ids=true, to_apply=%region_7.8 | all-reduce | flops 6144 | bytes 49152 | tf_op jit(solution)/shard_map/psum | solution.py:77
  140.9 0.0 copy-start.5
  141.0 0.0 copy-start.6
  141.0 1.4 slice_reduce_fusion.1
  142.4 0.0 copy-start.1
  142.4 0.0 copy-done.5
  142.4 0.0 copy-done.6
  142.5 1.0 gather_fusion.2
  143.5 0.1 broadcast_bitcast_fusion
  143.5 0.0 copy-done.1
  143.5 1.0 fusion.9
  144.5 0.6 dynamic_slice.11
  (16 shorter events, 0.2 us)
Async XLA Ops:
  7.2 38.3 %all-reduce.3.cloned.1.call-start = ((), (), s32[]{:S(2)}) async-start(), calls=%async_computation | async-start | bytes 262144 | tf_op jit(solution)/shard_map/psum | solution.py:62
  9.4 0.7 copy-start.3
  10.2 0.7 copy-start.7
  46.3 23.0 %copy-start = (f32[16384]{0:T(1024)S(1)}, f32[16384]{0:T(1024)}, u32[]{:S(2)}) copy-start(f32[16384]{0:T(1024)} %get-tuple-element.63) | copy-start | bytes 196612
  69.4 23.1 %copy-start.2 = (f32[32,128]{1,0:T(8,128)S(1)}, f32[32,128]{1,0:T(8,128)}, u32[]{:S(2)}) copy-start(f32[32,128]{1,0:T(8,128)} %param.11) | copy-start | bytes 49156
  69.4 23.1 %copy-start.4 = (f32[32,128]{1,0:T(8,128)S(1)}, f32[32,128]{1,0:T(8,128)}, u32[]{:S(2)}) copy-start(f32[32,128]{1,0:T(8,128)} %param.10) | copy-start | bytes 49156
  140.9 1.5 copy-start.5
  141.0 1.5 copy-start.6
  142.4 1.1 copy-start.1
Sparse Core Ops, SparseCore 0:
  10.9 34.5 all-reduce.2
where the time goes:
time: 152 us
  local copies, waits for them, and re-layouts  50.4 us (33%)
  blocking collectives  45.8 us (30%)
  waiting for transfers between devices  34.6 us (23%)
  between operations  14.3 us (9%)
  other arithmetic  5.59 us (4%)
    psum x1, blocking collectives, body(): totals = lax.psum(placed_sums, ('region', 'member'))  45.8 us
    psum x1, waiting for transfers between devices, body(): point_total, point_square = lax.psum((local_total, local_square), 'member')  34.6 us
    gather x1, local copies, waits for them, and re-layouts, body(): at_mean = point_mean[own_points]  23 us
    gather x1, local copies, waits for them, and re-layouts, body(): at_square = point_square[own_points]  23 us
  transfers between devices with their start and end apart: 1, of which 1 were waited for; matrix products, arithmetic and copies ran while one was open for 0% of the time, Pallas kernels for 0%

commit v1 on v0

--- a/solution.py
+++ b/solution.py
@@ -74,7 +74,7 @@
     share = num_blocks // lax.axis_size(("region", "member"))
     first = lax.axis_index(("region", "member")) * share
     placed_sums = jnp.zeros((6, num_blocks), jnp.float32).at[:, owned_blocks].set(slot_sums)
-    totals = lax.psum(placed_sums, ("region", "member"))
+    totals = lax.psum(lax.psum(placed_sums, "member"), "region")
     lambda_all = posterior(totals, infl_mean, infl_var)
     lambda_mine = lax.dynamic_slice_in_dim(lambda_all, first, share)
     lambda_owned = lambda_all[owned_blocks]

time: 152 us -> 166 us (1.092)
  blocking collectives: 45.8 us -> 59.4 us
    psum x1 -> x2, blocking collectives: 45.8 us -> 59.4 us  [body(): totals = lax.psum(lax.psum(placed_sums, 'member'), 'region')]
where the time goes in v1:
time: 166 us; the launch traced here: 165 us
  blocking collectives  59.4 us (36%)
  local copies, waits for them, and re-layouts  50.4 us (30%)
  waiting for transfers between devices  34.6 us (21%)
  between operations  14.3 us (9%)
  other arithmetic  5.59 us (3%)
    psum x2, blocking collectives, body(): totals = lax.psum(lax.psum(placed_sums, 'member'), 'region')  59.4 us
    psum x1, waiting for transfers between devices, body(): point_total, point_square = lax.psum((local_total, local_square), 'member')  34.6 us
    gather x1, local copies, waits for them, and re-layouts, body(): at_mean = point_mean[own_points]  23 us
    gather x1, local copies, waits for them, and re-layouts, body(): at_square = point_square[own_points]  23 us
  transfers between devices with their start and end apart: 1, of which 1 were waited for; matrix products, arithmetic and copies ran while one was open for 0% of the time, Pallas kernels for 0%

profile of v1, /device:TPU:0, one launch (start us, length us, event | category | flops | bytes accessed | tf_op | source)
XLA Modules:
  0.0 165.5 jit_solution(12511674251205361608)
XLA Ops:
  7.2 0.0 all-reduce.3.cloned.1.call-start
  7.2 2.2 %fusion.6 = (f32[16384]{0:T(1024)}, f32[16384]{0:T(1024)}) fusion(bf16[10,16384]{1,0:T(8,128)(2,1)} %param.9), kind=kLoop, calls=%fused_computation.15 | loop fusion | flops 622592 | bytes 458752 | tf_op jit(solution)/shard_map/reduce_sum | solution.py:60
  9.4 0.0 all-reduce.3.cloned.1.call-update
  9.4 0.7 copy-done.3
  10.2 0.0 copy-start.7
  10.2 0.6 copy-done.7
  10.9 34.6 %all-reduce.3.cloned.1.call-done = (f32[16384]{0:T(1024)}, f32[16384]{0:T(1024)}) async-done(((f32[16384]{0:T(1024)}, f32[16384]{0:T(1024)}), (f32[16384]{0:T(1024)}, f32[16384]{0:T(1024)})) %all-reduce.3.cloned.1.call-update) | async-done | bytes 131088 | tf_op jit(solution)/shard_map/psum | solution.py:62
  45.5 0.8 broadcast_multiply_fusion
  46.4 23.0 %gather_fusion = f32[4096]{0:T(1024)S(1)} fusion(f32[16384]{0:T(1024)S(1)} %broadcast_multiply_fusion, s32[4096]{0:T(1024)S(1)} %broadcast_clamp_fusion), kind=kCustom, calls=%fused_computation | custom fusion | bytes 49152 | tf_op jit(solution)/shard_map/gather | solution.py:65
  69.4 0.0 copy-done
  69.4 0.0 copy-start.2
  69.4 0.0 copy-start.4
  69.4 23.0 %gather_fusion.1 = f32[4096]{0:T(1024)S(1)} fusion(f32[16384]{0:T(1024)S(1)} %copy-done, s32[4096]{0:T(1024)S(1)} %broadcast_clamp_fusion), kind=kCustom, calls=%fused_computation.1 | custom fusion | bytes 49152 | tf_op jit(solution)/shard_map/gather | solution.py:64
  92.5 0.1 fusion.20
  92.6 0.2 stack.2
  92.7 1.2 while.11
  92.8 0.6 convolution_add_fusion.2
  93.4 0.6 convolution_add_fusion.2
  94.0 0.1 copy.10
  94.1 1.0 scatter_custom_fusion
  95.1 16.0 %psum.30 = f32[6,1024]{0,1:T(8,128)S(1)} all-reduce(f32[6,1024]{0,1:T(8,128)S(1)} %scatter_custom_fusion), channel_id=1, replica_groups=mesh['region'=8,'member'=4] {'member'}, use_global_device_ids=true, to_apply=%region_7.8 | all-reduce | flops 6144 | bytes 49152 | tf_op jit(solution)/shard_map/psum | solution.py:77
  111.2 43.3 %psum.31 = f32[6,1024]{0,1:T(8,128)S(1)} all-reduce(f32[6,1024]{0,1:T(8,128)S(1)} %psum.30), channel_id=1, replica_groups=mesh['region'=8,'member'=4] {'region'}, use_global_device_ids=true, to_apply=%region_8.9 | all-reduce | flops 6144 | bytes 49152 | tf_op jit(solution)/shard_map/psum | solution.py:77
  154.5 0.0 copy-start.5
  154.5 0.0 copy-start.6
  154.5 1.4 slice_reduce_fusion.1
  156.0 0.0 copy-start.1
  156.0 0.0 copy-done.5
  156.0 1.0 gather_fusion.2
  157.0 0.1 broadcast_bitcast_fusion
  157.1 0.0 copy-done.1
  157.1 1.0 fusion.9
  158.1 0.6 dynamic_slice.11
  (17 shorter events, 0.2 us)
Async XLA Ops:
  7.2 38.3 %all-reduce.3.cloned.1.call-start = ((), (), s32[]{:S(2)}) async-start(), calls=%async_computation | async-start | bytes 262144 | tf_op jit(solution)/shard_map/psum | solution.py:62
  9.4 0.7 copy-start.3
  10.2 0.7 copy-start.7
  46.3 23.0 %copy-start = (f32[16384]{0:T(1024)S(1)}, f32[16384]{0:T(1024)}, u32[]{:S(2)}) copy-start(f32[16384]{0:T(1024)} %get-tuple-element.63) | copy-start | bytes 196612
  69.4 23.1 %copy-start.2 = (f32[32,128]{1,0:T(8,128)S(1)}, f32[32,128]{1,0:T(8,128)}, u32[]{:S(2)}) copy-start(f32[32,128]{1,0:T(8,128)} %param.11) | copy-start | bytes 49156
  69.4 23.1 %copy-start.4 = (f32[32,128]{1,0:T(8,128)S(1)}, f32[32,128]{1,0:T(8,128)}, u32[]{:S(2)}) copy-start(f32[32,128]{1,0:T(8,128)} %param.10) | copy-start | bytes 49156
  154.5 1.5 copy-start.5
  154.5 1.5 copy-start.6
  156.0 1.1 copy-start.1
Sparse Core Ops, SparseCore 0:
  10.9 34.5 all-reduce.2
